TPU v7x, 32 devices: a whole 2x2x4 slice. The times are simulated.
32 devices in a mesh: row: 4 (over y, core), col: 8 (over z, x).
Axes of the slice: x: 2, y: 2, z: 4, core: 2. Of those that a mesh axis runs over, the one named last changes fastest.
Arguments:
- adjacency: int32 [3392, 3392], P('row', 'col'), may hold values from 0 to 3
- degree: int32 [3392], replicated, may hold values from 64 to 511
- cotangent: bfloat16 [3392, 512], P(('row', 'col')), may hold values from -6 to 6
- features: bfloat16 [3392, 512], P('col'), may hold values from -0.029907227 to 0.029907227
- weight: bfloat16 [512, 512], replicated, may hold values from -0.25 to 0.25
Outputs:
- grad_input: bfloat16 [3392, 512], P('col', 'row')
- grad_weight: float32 [512, 512], P('col', 'row')
All inputs are finite; a program needn't handle non-finite values.
Results may differ from a plain program's by a relative error of at most 0.0058.
Values may be sent and summed in bfloat16 or wider, within the bound.
A program may use at most 128 MiB of HBM per device.

v0:
```python
import jax
import jax.numpy as jnp
from jax import lax
from jax.sharding import PartitionSpec as P


def per_device(adjacency, degree, cotangent, features, weight):
    rows_here, cols_here = adjacency.shape
    row_index = lax.axis_index("row")
    col_index = lax.axis_index("col")
    inv_root = lax.rsqrt(degree.astype(jnp.float32))
    row_scale = lax.dynamic_slice_in_dim(inv_root, row_index * rows_here, rows_here, 0)
    col_scale = lax.dynamic_slice_in_dim(inv_root, col_index * cols_here, cols_here, 0)
    tile = adjacency.astype(jnp.bfloat16)
    width = weight.shape[0]
    scaled = (
        lax.all_gather(cotangent, "col", axis=0, tiled=True).astype(jnp.float32)
        * row_scale[:, None]
    ).astype(jnp.bfloat16)
    partial_sum = lax.dot_general(
        tile, scaled, (((0,), (0,)), ((), ())), preferred_element_type=jnp.float32
    )
    share = width // lax.axis_size("row")
    weight_rows = lax.dynamic_slice_in_dim(weight, row_index * share, share, 0)
    pieces = lax.psum_scatter(partial_sum, "row", scatter_dimension=1, tiled=True)
    z_columns = (pieces * col_scale[:, None]).astype(jnp.bfloat16)
    grad_z = lax.all_gather(z_columns, "row", axis=1, tiled=True)
    grad_input = lax.dot_general(
        grad_z, weight_rows, (((1,), (1,)), ((), ())), preferred_element_type=jnp.float32
    )
    weight_term = lax.dot_general(
        features, z_columns, (((0,), (0,)), ((), ())), preferred_element_type=jnp.float32
    )
    grad_weight = lax.psum_scatter(weight_term, "col", scatter_dimension=0, tiled=True)
    return (grad_input.astype(jnp.bfloat16), grad_weight)


def solution(mesh):
    placed = (P("row", "col"), P(), P(("row", "col"), None), P("col", None), P())
    return jax.shard_map(
        per_device,
        mesh=mesh,
        in_specs=placed,
        out_specs=(P("col", "row"), P("col", "row")),
        check_vma=False,
    )
```

profile of v0, /device:TPU:0, one launch (start us, length us, event | category | flops | bytes accessed | tf_op | source)
XLA Modules:
  0.0 142.8 jit_solution(9219729630339342434)
XLA Ops:
  7.2 0.0 copy-start
  7.2 0.0 reduce-scatter.5.cloned.1.call-start
  7.2 0.0 copy-start.2
  7.2 34.6 %all-gather = bf16[8,106,512]{2,1,0:T(8,128)(2,1)S(1)} all-gather(bf16[1,106,512]{2,1,0:T(8,128)(2,1)} %bitcast.9), channel_id=1, replica_groups=mesh['row'=4,'col'=8] {'col'}, dimensions={0}, use_global_device_ids=true | all-gather | bytes 976896 | tf_op jit(solution)/shard_map/all_gather | solution.py:17
  41.8 0.2 reshape.8
  42.0 0.0 copy-done.2
  42.0 0.1 dynamic_slice.9
  42.1 0.0 copy-start.1
  42.1 3.0 %convolution_bitcast_fusion = f32[424,512]{1,0:T(8,128)} fusion(f32[848,512]{1,0:T(8,128)S(1)} %reshape.8, f32[848]{0:T(1024)S(1)} %dynamic_slice.9, s32[848,424]{0,1:T(8,128)} %param.5), kind=kOutput, calls=%fused_computation.1 | convolution fusion | flops 369409152 | bytes 4046656 | tf_op jit(solution)/shard_map/dot_general | solution.py:20
  45.2 0.0 reduce-scatter.5.cloned.1.call-update
  45.2 0.0 reduce-scatter.7.cloned.1.call-start
  45.2 0.1 dynamic_slice.10
  45.3 24.6 %reduce-scatter.5.cloned.1.call-done = f32[424,128]{1,0:T(8,128)} async-done(((f32[424,512]{1,0:T(8,128)}), f32[424,128]{1,0:T(8,128)}) %reduce-scatter.5.cloned.1.call-update) | async-done | bytes 217104 | tf_op jit(solution)/shard_map/reduce_scatter | solution.py:25
  69.9 1.1 multiply_convert_fusion.2
  71.0 0.0 copy-done.1
  71.0 0.2 convolution_bitcast_fusion.1
  71.3 0.8 copy.10
  72.1 0.0 reduce-scatter.7.cloned.1.call-update
  72.1 6.3 %all_gather.7 = bf16[424,512]{1,0:T(8,128)(2,1)S(1)} all-gather(bf16[424,128]{1,0:T(8,128)(2,1)S(1)} %multiply_convert_fusion.2), channel_id=1, replica_groups=mesh['row'=4,'col'=8] {'row'}, dimensions={1}, use_global_device_ids=true | all-gather | bytes 542720 | tf_op jit(solution)/shard_map/all_gather | solution.py:27
  78.4 0.0 copy-done
  78.4 0.9 convolution_convert_fusion
  79.3 56.6 %reduce-scatter.7.cloned.1.call-done = f32[64,128]{1,0:T(8,128)} async-done(((f32[512,128]{1,0:T(8,128)}), f32[64,128]{1,0:T(8,128)}) %reduce-scatter.7.cloned.1.call-update) | async-done | bytes 32784
  (1 shorter events, 0.0 us)
Async XLA Ops:
  7.2 71.2 %copy-start = (bf16[512,512]{1,0:T(8,128)(2,1)S(1)}, bf16[512,512]{1,0:T(8,128)(2,1)}, u32[]{:S(2)}) copy-start(bf16[512,512]{1,0:T(8,128)(2,1)} %param.9) | copy-start | bytes 1572868
  7.2 62.8 %reduce-scatter.5.cloned.1.call-start = ((), (), s32[]{:S(2)}) async-start(), calls=%async_computation.2 | async-start | bytes 1085440 | tf_op jit(solution)/shard_map/reduce_scatter | solution.py:25
  7.2 34.8 %copy-start.2 = (s32[3392]{0:T(1024)S(1)}, s32[3392]{0:T(1024)}, u32[]{:S(2)}) copy-start(s32[3392]{0:T(1024)} %param.6) | copy-start | bytes 40708
  42.1 28.9 %copy-start.1 = (bf16[424,512]{1,0:T(8,128)(2,1)S(1)}, bf16[424,512]{1,0:T(8,128)(2,1)}, u32[]{:S(2)}) copy-start(bf16[424,512]{1,0:T(8,128)(2,1)} %param.8) | copy-start | bytes 1302532
  45.2 90.8 %reduce-scatter.7.cloned.1.call-start = ((), (), s32[]{:S(2)}) async-start(), calls=%async_computation.3 | async-start | bytes 294912
Sparse Core Ops, SparseCore 0:
  45.3 24.5 reduce-scatter.4
  73.8 62.0 reduce-scatter.6
where the time goes:
time: 143 us
  waiting for transfers between devices  81.3 us (57%)
  blocking collectives  40.8 us (29%)
  between operations  14.1 us (10%)
  matrix products  4.22 us (3%)
    unnamed x3, waiting for transfers between devices  56.7 us
    all_gather x1, blocking collectives, per_device(): lax.all_gather(cotangent, 'col', axis=0, tiled=True).astype(jnp.float32)  34.6 us
    reduce_scatter x1, waiting for transfers between devices, per_device(): lax.psum_scatter(partial_sum, 'row', scatter_dimension=1, tiled=True)  24.6 us
    all_gather x1, blocking collectives, per_device(): grad_z = lax.all_gather(z_columns, 'row', axis=1, tiled=True)  6.28 us
    dot_general x1, matrix products, per_device(): lax.dot_general(tile, scaled, (((0,), (0,)), ((), ())), preferred_element...  3.05 us
  transfers between devices with their start and end apart: 2, of which 2 were waited for; matrix products, arithmetic and copies ran while one was open for 1% of the time, Pallas kernels for 0%

commit v1 on v0

v1 whole, which is shorter than its diff:
```python
import functools

import jax
import jax.numpy as jnp
from jax import lax
from jax.experimental import pallas as pl
from jax.experimental.pallas import tpu as pltpu
from jax.sharding import PartitionSpec as P

MESH = pl.DeviceIdType.MESH
F32, BF16 = jnp.float32, jnp.bfloat16
CORES = 2


def up(size, unit):
    return -(-size // unit) * unit


def inner_of(count):
    return max(d for d in range(1, count + 1) if count % d == 0 and d * d <= count)


def kernel(
    R, C, block,
    x_ref, a_hbm, f_hbm, w_hbm, scale_ref, gi_ref, gw_ref,
    a_v, f_v, w_v, at, ft, s_v, mine, part, theirs, z_all, wt, wrec,
    load_sem, swap_sem, own_sem, pair_sem, got_sem, fwd_sem,
    part_send, part_recv, z_send, z_recv, z_fwd, wt_send, wt_recv,
):
    I = inner_of(C)
    O = C // I
    Y = R // CORES
    rows, n = a_v.shape
    padded, share = x_ref.shape[1:]
    slot = s_v.shape[3]
    r = lax.axis_index("row")
    c = lax.axis_index("col")
    y, k = r // CORES, r % CORES
    o, i = c // I, c % I
    mate = y * CORES + (1 - k)
    outer = [lax.rem(o + d, O) * I + i for d in range(1, O)]
    inner = [o * I + lax.rem(i + d, I) for d in range(1, I)]
    others = [lax.rem(c + d, C) for d in range(1, C)]
    y_at = [lax.rem(y + 1 + s, Y) for s in range(Y)]

    def remote(src, dst, send, recv, row, col):
        return pltpu.make_async_remote_copy(
            src_ref=src, dst_ref=dst, send_sem=send, recv_sem=recv,
            device_id=(row, col), device_id_type=MESH,
        )

    def await_bytes(ref, sem):
        pltpu.make_async_copy(ref, ref, sem).wait()

    load_a = pltpu.make_async_copy(a_hbm, a_v, load_sem.at[0])
    load_f = pltpu.make_async_copy(f_hbm, f_v, load_sem.at[1])
    load_w = pltpu.make_async_copy(
        w_hbm.at[pl.ds(pl.multiple_of(r * share, share), share), :], w_v, load_sem.at[2]
    )
    load_a.start()
    load_f.start()
    load_w.start()

    barrier = pltpu.get_barrier_semaphore()
    peers = [(r, p) for p in others] + [(mate, p) for p in outer + inner] + [(mate, c)]
    peers += [(yy * CORES + k, c) for yy in y_at[:-1]]
    for row, col in peers:
        pl.semaphore_signal(barrier, inc=1, device_id=(row, col), device_id_type=MESH)
    pl.semaphore_wait(barrier, len(peers))

    live = pl.ds(0, padded)
    for s in range(Y):
        same = x_ref.at[y_at[s] * CORES + k]
        cross = x_ref.at[y_at[s] * CORES + (1 - k)]
        for p in outer + inner:
            remote(same, s_v.at[s, 0, c, live], own_sem.at[s, 0], got_sem.at[s, c], r, p).start()
            remote(cross, s_v.at[s, 1, c, live], own_sem.at[s, 1], got_sem.at[s, c], mate, p).start()
        remote(cross, s_v.at[s, 1, c, live], pair_sem.at[s], got_sem.at[s, c], mate, c).start()
        s_v[s, 0, c, 0:padded, :] = x_ref[y_at[s] * CORES + k]
    if slot > padded:
        for s in range(Y):
            s_v[s, :, :, padded:slot, :] = jnp.zeros((CORES, C, slot - padded, share), BF16)

    load_a.wait()
    for j in range(C):
        tile = a_v[j * block:(j + 1) * block, :].astype(F32)
        if slot > block:
            tile = jnp.concatenate([tile, jnp.zeros((slot - block, n), F32)], axis=0)
        at[0, :, j * slot:(j + 1) * slot] = tile.T.astype(BF16)
    swap = remote(at.at[0], at.at[1], swap_sem.at[0], swap_sem.at[1], mate, c)
    swap.start()
    load_f.wait()
    ft[...] = f_v[...].astype(F32).T.astype(BF16)

    group = min(C, 8)

    def forward(s):
        for d, p in enumerate(outer):
            await_bytes(s_v.at[s, :, p, live], got_sem.at[s, p])
            for q in inner:
                remote(
                    s_v.at[s, :, p, live], s_v.at[s, :, p, live],
                    fwd_sem.at[s, d], got_sem.at[s, p], r, q,
                ).start()

    def gathered(s):
        await_bytes(s_v.at[s, 1, c, live], got_sem.at[s, c])
        for e in range(1, I):
            for d in range(O):
                p = lax.rem(o + d, O) * I + lax.rem(i + e, I)
                await_bytes(s_v.at[s, :, p, live], got_sem.at[s, p])

    def product(s):
        def term(t, g):
            left = at[t, :, pl.ds(pl.multiple_of(g * group * slot, group * slot), group * slot)]
            right = s_v[s, t, pl.ds(g * group, group)].reshape(group * slot, share)
            return jnp.dot(left, right, preferred_element_type=F32)

        if C == group:
            mine[...] = term(0, 0) + term(1, 0)
        else:
            mine[...] = jnp.zeros_like(mine)

            @pl.loop(0, C // group)
            def _(g):
                mine[...] += term(0, g) + term(1, g)

    for s in range(Y):
        forward(s)
        gathered(s)
        if s == 0:
            swap.wait()
        product(s)
        if s < Y - 1:
            part[s] = mine[...]
            remote(
                part.at[s], theirs.at[s], part_send.at[s], part_recv.at[s], y_at[s] * CORES + k, c
            ).start()

    total = mine[...]
    for s in range(Y - 1):
        await_bytes(theirs.at[s], part_recv.at[s])
        total = total + theirs[s]
    z_mine = (total * scale_ref[...]).astype(BF16)
    z_all[r] = z_mine
    z_here = z_all.at[r]
    for s in range(Y - 1):
        remote(z_here, z_here, z_send.at[s], z_recv.at[r], y_at[s] * CORES + k, c).start()
    remote(z_here, z_here, z_send.at[Y - 1], z_recv.at[r], mate, c).start()

    term = jnp.dot(ft[...], z_mine, preferred_element_type=F32)
    wt[...] = term.reshape(wt.shape)
    for p in others:
        remote(wt.at[p], wrec.at[c], wt_send.at[0], wt_recv.at[c], r, p).start()

    for s in range(Y - 1):
        q = y_at[s] * CORES + k
        await_bytes(z_all.at[q], z_recv.at[q])
        remote(z_all.at[q], z_all.at[q], z_fwd.at[s], z_recv.at[q], mate, c).start()
    load_w.wait()
    for s in range(Y):
        q = y_at[s] * CORES + (1 - k)
        await_bytes(z_all.at[q], z_recv.at[q])
    out = jnp.zeros((n, share), F32)
    for q in range(R):
        out = out + lax.dot_general(
            z_all[q], w_v[:, q * share:(q + 1) * share],
            (((1,), (1,)), ((), ())), preferred_element_type=F32,
        )
    gi_ref[...] = out.astype(BF16)

    gw = wt[c]
    for p in others:
        await_bytes(wrec.at[p], wt_recv.at[p])
        gw = gw + wrec[p]
    gw_ref[...] = gw

    for s in range(Y):
        for t in range(CORES):
            await_bytes(s_v.at[s, t, pl.ds(0, O - 1 + I - 1), live], own_sem.at[s, t])
        await_bytes(s_v.at[s, 1, 0, live], pair_sem.at[s])
        if I > 1:
            for d in range(O - 1):
                await_bytes(s_v.at[s, :, pl.ds(0, I - 1), live], fwd_sem.at[s, d])
    for s in range(Y - 1):
        await_bytes(part.at[s], part_send.at[s])
        await_bytes(z_here, z_fwd.at[s])
    for s in range(Y):
        await_bytes(z_here, z_send.at[s])
    await_bytes(wt.at[pl.ds(0, C - 1)], wt_send.at[0])


def per_device(R, C, adjacency, degree, cotangent, features, weight):
    rows, n = adjacency.shape
    block, width = cotangent.shape
    share = width // R
    padded, slot = up(block, 16), up(block, 128)
    I = inner_of(C)
    O, Y = C // I, R // CORES
    row_index, col_index = lax.axis_index("row"), lax.axis_index("col")
    inv_root = lax.rsqrt(degree.astype(F32))
    row_scale = lax.dynamic_slice_in_dim(inv_root, row_index * rows + col_index * block, block, 0)
    col_scale = lax.dynamic_slice_in_dim(inv_root, col_index * n, n, 0)
    scaled = (cotangent.astype(F32) * row_scale[:, None]).astype(BF16)
    scaled = jnp.pad(scaled, ((0, padded - block), (0, 0)))
    pieces = scaled.reshape(padded, R, share).transpose(1, 0, 2)
    vmem = pl.BlockSpec(memory_space=pltpu.VMEM)
    hbm = pl.BlockSpec(memory_space=pl.ANY)
    dma = pltpu.SemaphoreType.DMA
    return pl.pallas_call(
        functools.partial(kernel, R, C, block),
        out_shape=(
            jax.ShapeDtypeStruct((n, width // R), BF16),
            jax.ShapeDtypeStruct((width // C, share), F32),
        ),
        in_specs=[vmem, hbm, hbm, hbm, vmem],
        out_specs=(vmem, vmem),
        scratch_shapes=[
            pltpu.VMEM((rows, n), jnp.int32),
            pltpu.VMEM((n, width), BF16),
            pltpu.VMEM((share, width), BF16),
            pltpu.VMEM((CORES, n, C * slot), BF16),
            pltpu.VMEM((width, n), BF16),
            pltpu.VMEM((Y, CORES, C, slot, share), BF16),
            pltpu.VMEM((n, share), F32),
            pltpu.VMEM((max(Y - 1, 1), n, share), F32),
            pltpu.VMEM((max(Y - 1, 1), n, share), F32),
            pltpu.VMEM((R, n, share), BF16),
            pltpu.VMEM((C, width // C, share), F32),
            pltpu.VMEM((C, width // C, share), F32),
            dma((3,)),
            dma((2,)),
            dma((Y, CORES)),
            dma((Y,)),
            dma((Y, C)),
            dma((Y, max(O - 1, 1))),
            dma((max(Y - 1, 1),)),
            dma((max(Y - 1, 1),)),
            dma((Y,)),
            dma((R,)),
            dma((max(Y - 1, 1),)),
            dma((1,)),
            dma((C,)),
        ],
        compiler_params=pltpu.CompilerParams(
            collective_id=0, has_side_effects=True, vmem_limit_bytes=60 * 1024 * 1024
        ),
    )(pieces, adjacency, features, weight, col_scale[:, None])


def solution(mesh):
    placed = (P("row", "col"), P(), P(("row", "col"), None), P("col", None), P())
    return jax.shard_map(
        functools.partial(per_device, mesh.shape["row"], mesh.shape["col"]),
        mesh=mesh,
        in_specs=placed,
        out_specs=(P("col", "row"), P("col", "row")),
        check_vma=False,
    )
```

time: 143 us -> 44.3 us (0.31)
  waiting for transfers between devices: 81.3 us -> 0 us
  blocking collectives: 40.8 us -> 0 us
  Pallas kernels: 0 us -> 34.3 us
  between operations: 14.1 us -> 0.66 us
  local copies, waits for them, and re-layouts: 1.2 us -> 7.34 us
  matrix products: 4.22 us -> 0 us
    unnamed x3 -> x0, waiting for transfers between devices: 56.7 us -> none
    all_gather x2 -> x0, blocking collectives: 40.8 us -> none  [the longest x1 34.6 us: per_device(): lax.all_gather(cotangent, 'col', axis=0, tiled=True).astype(jnp.float32)]
    pallas_call x0 -> x1, Pallas kernels: none -> 34.3 us  [per_device(): pl.pallas_call(functools.partial(kernel, R, C, block), out_shape=(jax.Sha...]
    reduce_scatter x1 -> x0, waiting for transfers between devices: 24.6 us -> none  [per_device(): lax.psum_scatter(partial_sum, 'row', scatter_dimension=1, tiled=True)]
    unnamed x7 -> x3, local copies, waits for them, and re-layouts: 0.84 us -> 5.69 us
    dot_general x3 -> x0, matrix products: 4.22 us -> none  [the longest x1 3.05 us: per_device(): lax.dot_general(tile, scaled, (((0,), (0,)), ((), ())), preferred_element...]
  transfers between devices with their start and end apart: 2 -> 0, of which waited for: 2 -> 0; matrix products, arithmetic and copies ran while one was open for 1% -> 0% of each run, Pallas kernels for 0% -> 0%
where the time goes in v1:
time: 44.3 us; the launch traced here: 44 us
  Pallas kernels  34.3 us (77%)
  local copies, waits for them, and re-layouts  7.34 us (17%)
  other arithmetic  1.71 us (4%)
  between operations  0.66 us (1%)
    pallas_call x1, Pallas kernels, per_device(): pl.pallas_call(functools.partial(kernel, R, C, block), out_shape=(jax.Sha...  34.3 us
    unnamed x3, local copies, waits for them, and re-layouts  5.69 us
    convert_element_type x1, other arithmetic, per_device(): scaled = (cotangent.astype(F32) * row_scale[:, None]).astype(BF16)  0.98 us

profile of v1, /device:TPU:0, one launch (start us, length us, event | category | flops | bytes accessed | tf_op | source)
XLA Modules:
  0.0 44.0 jit_solution(13088174953834144955)
XLA Ops:
  0.6 0.7 %convert_rsqrt_fusion = f32[3392]{0:T(1024)S(1)} fusion(s32[3392]{0:T(1024)} %param.6), kind=kLoop, calls=%fused_computation.3 | loop fusion | flops 3392 | bytes 27136 | tf_op jit(solution)/shard_map/rsqrt | solution.py:201
  1.4 0.1 dynamic_slice.6
  1.4 0.1 dynamic_slice.7
  1.5 1.0 %multiply_convert_fusion = bf16[106,512]{1,0:T(8,128)(2,1)S(1)} fusion(bf16[106,512]{1,0:T(8,128)(2,1)} %param.7, f32[106]{0:T(128)S(1)} %dynamic_slice.6), kind=kLoop, calls=%fused_computation | loop fusion | flops 162816 | bytes 217512 | tf_op jit(solution)/shard_map/convert_element_type | solution.py:204
  2.5 0.7 %bitcast_bitcast_fusion.x_ref = bf16[4,112,128]{2,1,0:T(8,128)(2,1)} fusion(bf16[106,512]{1,0:T(8,128)(2,1)S(1)} %multiply_convert_fusion), kind=kLoop, calls=%fused_computation.1 | loop fusion | bytes 223232 | tf_op jit(solution)/shard_map/transpose | solution.py:206
  3.2 0.8 %copy.10.scale_ref = f32[424,1]{1,0:T(8,128)} copy(f32[424,1]{0,1:T(1,128)S(1)} %bitcast.8) | data formatting | bytes 3392 | tf_op jit(solution)/shard_map/broadcast_in_dim | solution.py:248
  4.0 2.8 %copy.9.a_hbm = s32[848,424]{1,0:T(8,128)} copy(s32[848,424]{0,1:T(8,128)} %param.5) | data formatting | bytes 2876416 | tf_op args[0]
  6.8 34.3 %shard_map.68 = (bf16[424,128]{1,0:T(8,128)(2,1)}, f32[64,128]{1,0:T(8,128)}) custom-call(bf16[4,112,128]{2,1,0:T(8,128)(2,1)} %bitcast_bitcast_fusion.x_ref, s32[848,424]{1,0:T(8,128)} %copy.9.a_hbm, bf16[424,512]{1,0:T(8,128)(2,1)} %f_hbm.1, bf16[512,512]{1,0:T(8,128)(2,1)} %w_hbm.1, f32[424,1]{1,0:T(8,128)} %copy.10.scale_ref), custom_call_target="tpu_custom_call" | custom-call | tf_op jit(solution)/shard_map/pallas_call | solution.py:210
  41.1 1.5 %copy.15 = bf16[424,128]{1,0:T(8,128)(2,1)} copy(bf16[424,128]{1,0:T(8,128)(2,1)} %get-tuple-element.4) | data formatting | bytes 217088
  42.6 1.4 %copy.16 = f32[64,128]{1,0:T(8,128)} copy(f32[64,128]{1,0:T(8,128)} %get-tuple-element.5) | data formatting | bytes 65536

commit v2 on v1

--- a/solution.py
+++ b/solution.py
@@ -22,15 +22,15 @@
 
 def kernel(
     R, C, block,
-    x_ref, a_hbm, f_hbm, w_hbm, scale_ref, gi_ref, gw_ref,
-    a_v, f_v, w_v, at, ft, s_v, mine, part, theirs, z_all, wt, wrec,
+    cot_ref, degree_ref, a_hbm, f_hbm, w_hbm, gi_ref, gw_ref,
+    d_v, x_ref, a_v, f_v, w_v, at, ft, s_v, mine, part, theirs, z_all, wt, wrec,
     load_sem, swap_sem, own_sem, pair_sem, got_sem, fwd_sem,
     part_send, part_recv, z_send, z_recv, z_fwd, wt_send, wt_recv,
 ):
     I = inner_of(C)
     O = C // I
     Y = R // CORES
-    rows, n = a_v.shape
+    n, rows = a_v.shape
     padded, share = x_ref.shape[1:]
     slot = s_v.shape[3]
     r = lax.axis_index("row")
@@ -61,11 +61,29 @@
     load_f.start()
     load_w.start()
 
+    nodes = degree_ref.shape[1]
+
+    def scale_column(first, count):
+        start = pl.multiple_of(first // 128 * 128, 128)
+        span = up(count + 127, 128)
+        window = jnp.broadcast_to(d_v[:, pl.ds(start, span)], (up(count, 8), span))
+        lane = lax.broadcasted_iota(jnp.int32, window.shape, 1)
+        row = lax.broadcasted_iota(jnp.int32, window.shape, 0)
+        picked = jnp.where(lane - row == first - start, window, 0.0)
+        return jnp.sum(picked, axis=1, keepdims=True)[:count]
+
     barrier = pltpu.get_barrier_semaphore()
     peers = [(r, p) for p in others] + [(mate, p) for p in outer + inner] + [(mate, c)]
     peers += [(yy * CORES + k, c) for yy in y_at[:-1]]
     for row, col in peers:
         pl.semaphore_signal(barrier, inc=1, device_id=(row, col), device_id_type=MESH)
+    d_v[:, 0:nodes] = lax.rsqrt(degree_ref[...].astype(F32))
+    row_scale = scale_column(r * rows + c * block, block)
+    for q in range(R):
+        piece = cot_ref[:, q * share:(q + 1) * share].astype(F32) * row_scale
+        if padded > block:
+            piece = jnp.concatenate([piece, jnp.zeros((padded - block, share), F32)], axis=0)
+        x_ref[q] = piece.astype(BF16)
     pl.semaphore_wait(barrier, len(peers))
 
     live = pl.ds(0, padded)
@@ -83,14 +101,13 @@
 
     load_a.wait()
     for j in range(C):
-        tile = a_v[j * block:(j + 1) * block, :].astype(F32)
-        if slot > block:
-            tile = jnp.concatenate([tile, jnp.zeros((slot - block, n), F32)], axis=0)
-        at[0, :, j * slot:(j + 1) * slot] = tile.T.astype(BF16)
+        start = min(j * block, rows - slot)
+        tile = a_v[:, start:start + slot]
+        if j * block > start:
+            tile = pltpu.roll(tile, slot - (j * block - start), 1)
+        at[0, :, j * slot:(j + 1) * slot] = tile.astype(F32).astype(BF16)
     swap = remote(at.at[0], at.at[1], swap_sem.at[0], swap_sem.at[1], mate, c)
     swap.start()
-    load_f.wait()
-    ft[...] = f_v[...].astype(F32).T.astype(BF16)
 
     group = min(C, 8)
 
@@ -127,6 +144,10 @@
 
     for s in range(Y):
         forward(s)
+        if s == 0:
+            load_f.wait()
+            ft[...] = f_v[...].astype(F32).T.astype(BF16)
+            col_scale = scale_column(c * n, n)
         gathered(s)
         if s == 0:
             swap.wait()
@@ -141,7 +162,7 @@
     for s in range(Y - 1):
         await_bytes(theirs.at[s], part_recv.at[s])
         total = total + theirs[s]
-    z_mine = (total * scale_ref[...]).astype(BF16)
+    z_mine = (total * col_scale).astype(BF16)
     z_all[r] = z_mine
     z_here = z_all.at[r]
     for s in range(Y - 1):
@@ -193,19 +214,12 @@
 def per_device(R, C, adjacency, degree, cotangent, features, weight):
     rows, n = adjacency.shape
     block, width = cotangent.shape
-    share = width // R
+    nodes, share = degree.shape[0], width // R
     padded, slot = up(block, 16), up(block, 128)
     I = inner_of(C)
     O, Y = C // I, R // CORES
-    row_index, col_index = lax.axis_index("row"), lax.axis_index("col")
-    inv_root = lax.rsqrt(degree.astype(F32))
-    row_scale = lax.dynamic_slice_in_dim(inv_root, row_index * rows + col_index * block, block, 0)
-    col_scale = lax.dynamic_slice_in_dim(inv_root, col_index * n, n, 0)
-    scaled = (cotangent.astype(F32) * row_scale[:, None]).astype(BF16)
-    scaled = jnp.pad(scaled, ((0, padded - block), (0, 0)))
-    pieces = scaled.reshape(padded, R, share).transpose(1, 0, 2)
     vmem = pl.BlockSpec(memory_space=pltpu.VMEM)
-    hbm = pl.BlockSpec(memory_space=pl.ANY)
+    hbm = pl.BlockSpec(memory_space=pltpu.HBM)
     dma = pltpu.SemaphoreType.DMA
     return pl.pallas_call(
         functools.partial(kernel, R, C, block),
@@ -213,10 +227,12 @@
             jax.ShapeDtypeStruct((n, width // R), BF16),
             jax.ShapeDtypeStruct((width // C, share), F32),
         ),
-        in_specs=[vmem, hbm, hbm, hbm, vmem],
+        in_specs=[vmem, vmem, hbm, hbm, hbm],
         out_specs=(vmem, vmem),
         scratch_shapes=[
-            pltpu.VMEM((rows, n), jnp.int32),
+            pltpu.VMEM((1, up(nodes, 128) + up(n + 127, 128)), F32),
+            pltpu.VMEM((R, padded, share), BF16),
+            pltpu.VMEM((n, rows), jnp.int32),
             pltpu.VMEM((n, width), BF16),
             pltpu.VMEM((share, width), BF16),
             pltpu.VMEM((CORES, n, C * slot), BF16),
@@ -243,9 +259,9 @@
             dma((C,)),
         ],
         compiler_params=pltpu.CompilerParams(
-            collective_id=0, has_side_effects=True, vmem_limit_bytes=60 * 1024 * 1024
+            collective_id=0, has_side_effects=True, vmem_limit_bytes=min(60 << 20, (12 << 20) + 24 * rows * n)
         ),
-    )(pieces, adjacency, features, weight, col_scale[:, None])
+    )(cotangent, degree.reshape(1, nodes), adjacency.T, features, weight)
 
 
 def solution(mesh):

time: 44.3 us -> 41 us (0.926)
  other arithmetic: 1.71 us -> 0 us
  local copies, waits for them, and re-layouts: 7.34 us -> 6.32 us
  Pallas kernels: 34.3 us -> 33.4 us
    convert_element_type x1 -> x0, other arithmetic: 0.98 us -> none  [per_device(): scaled = (cotangent.astype(F32) * row_scale[:, None]).astype(BF16)]
    pallas_call x1, Pallas kernels: 34.3 us -> 33.4 us  [per_device(): pl.pallas_call(functools.partial(kernel, R, C, block), out_shape=(jax.Sha...]
    broadcast_in_dim x1 -> x0, local copies, waits for them, and re-layouts: 0.82 us -> none  [per_device(): col_scale[:, None]]
    reshape x0 -> x1, local copies, waits for them, and re-layouts: none -> 0.73 us  [per_device(): degree.reshape(1, nodes)]
    rsqrt x1 -> x0, other arithmetic: 0.72 us -> none  [per_device(): inv_root = lax.rsqrt(degree.astype(F32))]
    transpose x1 -> x0, local copies, waits for them, and re-layouts: 0.68 us -> none  [per_device(): pieces = scaled.reshape(padded, R, share).transpose(1, 0, 2)]
    unnamed x3 -> x10, local copies, waits for them, and re-layouts: 5.69 us -> 5.59 us
where the time goes in v2:
time: 41 us; the launch traced here: 40.4 us
  Pallas kernels  33.4 us (81%)
  local copies, waits for them, and re-layouts  6.32 us (15%)
  between operations  0.65 us (2%)
    pallas_call x1, Pallas kernels, per_device(): pl.pallas_call(functools.partial(kernel, R, C, block), out_shape=(jax.Sha...  33.4 us
    unnamed x10, local copies, waits for them, and re-layouts  5.59 us

profile of v2, /device:TPU:0, one launch (start us, length us, event | category | flops | bytes accessed | tf_op | source)
XLA Modules:
  0.0 40.4 jit_solution(456902432880340446)
XLA Ops:
  0.6 0.7 %reshape.7.degree_ref = s32[1,3392]{1,0:T(1,128)S(1)} reshape(s32[3392]{0:T(1024)} %param.6) | data formatting | bytes 27136 | tf_op jit(solution)/shard_map/reshape | solution.py:264
  1.4 0.0 copy-start
  1.4 1.4 %copy-done = s32[848,424]{0,1:T(8,128)S(1)} copy-done((s32[848,424]{0,1:T(8,128)S(1)}, s32[848,424]{0,1:T(8,128)}, u32[]{:S(2)}) %copy-start) | copy-done | bytes 1438232
  2.8 0.0 copy-start.1
  2.8 1.0 %copy-done.1 = bf16[512,512]{1,0:T(8,128)(2,1)S(1)} copy-done((bf16[512,512]{1,0:T(8,128)(2,1)S(1)}, bf16[512,512]{1,0:T(8,128)(2,1)}, u32[]{:S(2)}) %copy-start.1) | copy-done | bytes 524312
  3.8 0.0 copy-start.2
  3.8 1.0 %copy-done.2 = bf16[424,512]{1,0:T(8,128)(2,1)S(1)} copy-done((bf16[424,512]{1,0:T(8,128)(2,1)S(1)}, bf16[424,512]{1,0:T(8,128)(2,1)}, u32[]{:S(2)}) %copy-start.2) | copy-done | bytes 434200
  4.8 0.0 copy-start.3
  4.8 0.9 %copy-done.3 = bf16[106,512]{1,0:T(8,128)(2,1)S(1)} copy-done((bf16[106,512]{1,0:T(8,128)(2,1)S(1)}, bf16[106,512]{1,0:T(8,128)(2,1)}, u32[]{:S(2)}) %copy-start.3) | copy-done | bytes 108568
  5.7 33.4 %shard_map.68 = (bf16[424,128]{1,0:T(8,128)(2,1)S(1)}, f32[64,128]{1,0:T(8,128)S(1)}) custom-call(bf16[106,512]{1,0:T(8,128)(2,1)S(1)} %copy-done.3, s32[1,3392]{1,0:T(1,128)S(1)} %reshape.7.degree_ref, s32[424,848]{1,0:T(8,128)S(1)} %bitcast.1, bf16[424,512]{1,0:T(8,128)(2,1)S(1)} %copy-done.2, bf16[512,512]{1,0:T(8,128)(2,1)S(1)} %copy-done.1), custom_call_target="tpu_custom_call" | custom-call | tf_op jit(solution)/shard_map/pallas_call | solution.py:224
  39.1 0.6 %copy.9 = bf16[424,128]{1,0:T(8,128)(2,1)} copy(bf16[424,128]{1,0:T(8,128)(2,1)S(1)} %get-tuple-element.4) | data formatting | bytes 217088
  39.8 0.6 %copy.10 = f32[64,128]{1,0:T(8,128)} copy(f32[64,128]{1,0:T(8,128)S(1)} %get-tuple-element.5) | data formatting | bytes 65536
Async XLA Ops:
  1.4 1.4 %copy-start = (s32[848,424]{0,1:T(8,128)S(1)}, s32[848,424]{0,1:T(8,128)}, u32[]{:S(2)}) copy-start(s32[848,424]{0,1:T(8,128)} %param.5) | copy-start | bytes 4314628
  2.8 1.0 %copy-start.1 = (bf16[512,512]{1,0:T(8,128)(2,1)S(1)}, bf16[512,512]{1,0:T(8,128)(2,1)}, u32[]{:S(2)}) copy-start(bf16[512,512]{1,0:T(8,128)(2,1)} %w_hbm.1) | copy-start | bytes 1572868
  3.8 1.0 %copy-start.2 = (bf16[424,512]{1,0:T(8,128)(2,1)S(1)}, bf16[424,512]{1,0:T(8,128)(2,1)}, u32[]{:S(2)}) copy-start(bf16[424,512]{1,0:T(8,128)(2,1)} %f_hbm.1) | copy-start | bytes 1302532
  4.8 0.9 %copy-start.3 = (bf16[106,512]{1,0:T(8,128)(2,1)S(1)}, bf16[106,512]{1,0:T(8,128)(2,1)}, u32[]{:S(2)}) copy-start(bf16[106,512]{1,0:T(8,128)(2,1)} %cot_ref.1) | copy-start | bytes 325636

commit v3 on v2

--- a/solution.py
+++ b/solution.py
@@ -22,8 +22,8 @@
 
 def kernel(
     R, C, block,
-    cot_ref, degree_ref, a_hbm, f_hbm, w_hbm, gi_ref, gw_ref,
-    d_v, x_ref, a_v, f_v, w_v, at, ft, s_v, mine, part, theirs, z_all, wt, wrec,
+    cot_hbm, degree_ref, a_hbm, f_hbm, w_hbm, gi_ref, gw_ref,
+    d_v, cot_ref, x_ref, a_v, f_v, w_v, at, ft, s_v, mine, part, theirs, z_all, wt, wrec,
     load_sem, swap_sem, own_sem, pair_sem, got_sem, fwd_sem,
     part_send, part_recv, z_send, z_recv, z_fwd, wt_send, wt_recv,
 ):
@@ -57,6 +57,8 @@
     load_w = pltpu.make_async_copy(
         w_hbm.at[pl.ds(pl.multiple_of(r * share, share), share), :], w_v, load_sem.at[2]
     )
+    load_c = pltpu.make_async_copy(cot_hbm, cot_ref, load_sem.at[3])
+    load_c.start()
     load_a.start()
     load_f.start()
     load_w.start()
@@ -78,6 +80,7 @@
     for row, col in peers:
         pl.semaphore_signal(barrier, inc=1, device_id=(row, col), device_id_type=MESH)
     d_v[:, 0:nodes] = lax.rsqrt(degree_ref[...].astype(F32))
+    load_c.wait()
     row_scale = scale_column(r * rows + c * block, block)
     for q in range(R):
         piece = cot_ref[:, q * share:(q + 1) * share].astype(F32) * row_scale
@@ -218,6 +221,7 @@
     padded, slot = up(block, 16), up(block, 128)
     I = inner_of(C)
     O, Y = C // I, R // CORES
+    results = up(n, 16) * up(share, 128) * 2 + up(width // C, 8) * up(share, 128) * 4
     vmem = pl.BlockSpec(memory_space=pltpu.VMEM)
     hbm = pl.BlockSpec(memory_space=pltpu.HBM)
     dma = pltpu.SemaphoreType.DMA
@@ -227,10 +231,11 @@
             jax.ShapeDtypeStruct((n, width // R), BF16),
             jax.ShapeDtypeStruct((width // C, share), F32),
         ),
-        in_specs=[vmem, vmem, hbm, hbm, hbm],
+        in_specs=[hbm, vmem, hbm, hbm, hbm],
         out_specs=(vmem, vmem),
         scratch_shapes=[
             pltpu.VMEM((1, up(nodes, 128) + up(n + 127, 128)), F32),
+            pltpu.VMEM((block, width), BF16),
             pltpu.VMEM((R, padded, share), BF16),
             pltpu.VMEM((n, rows), jnp.int32),
             pltpu.VMEM((n, width), BF16),
@@ -244,7 +249,7 @@
             pltpu.VMEM((R, n, share), BF16),
             pltpu.VMEM((C, width // C, share), F32),
             pltpu.VMEM((C, width // C, share), F32),
-            dma((3,)),
+            dma((4,)),
             dma((2,)),
             dma((Y, CORES)),
             dma((Y,)),
@@ -259,7 +264,7 @@
             dma((C,)),
         ],
         compiler_params=pltpu.CompilerParams(
-            collective_id=0, has_side_effects=True, vmem_limit_bytes=min(60 << 20, (12 << 20) + 24 * rows * n)
+            collective_id=0, has_side_effects=True, vmem_limit_bytes=56300000
         ),
     )(cotangent, degree.reshape(1, nodes), adjacency.T, features, weight)
 

time: 41 us -> 35.9 us (0.88)
  local copies, waits for them, and re-layouts: 6.32 us -> 1.99 us
  Pallas kernels: 33.4 us -> 32.7 us
    unnamed x10 -> x2, local copies, waits for them, and re-layouts: 5.59 us -> 1.26 us
    pallas_call x1, Pallas kernels: 33.4 us -> 32.7 us  [per_device(): pl.pallas_call(functools.partial(kernel, R, C, block), out_shape=(jax.Sha...]
where the time goes in v3:
time: 35.9 us; the launch traced here: 35.4 us
  Pallas kernels  32.7 us (91%)
  local copies, waits for them, and re-layouts  1.99 us (6%)
  between operations  0.64 us (2%)
    pallas_call x1, Pallas kernels, per_device(): pl.pallas_call(functools.partial(kernel, R, C, block), out_shape=(jax.Sha...  32.7 us
    unnamed x2, local copies, waits for them, and re-layouts  1.26 us
    reshape x1, local copies, waits for them, and re-layouts, per_device(): degree.reshape(1, nodes)  0.73 us

profile of v3, /device:TPU:0, one launch (start us, length us, event | category | flops | bytes accessed | tf_op | source)
XLA Modules:
  0.0 35.4 jit_solution(7970951818270327201)
XLA Ops:
  0.6 0.7 %reshape.7.degree_ref = s32[1,3392]{1,0:T(1,128)S(1)} reshape(s32[3392]{0:T(1024)} %param.6) | data formatting | bytes 27136 | tf_op jit(solution)/shard_map/reshape | solution.py:269
  1.4 32.7 %shard_map.68 = (bf16[424,128]{1,0:T(8,128)(2,1)S(1)}, f32[64,128]{1,0:T(8,128)S(1)}) custom-call(bf16[106,512]{1,0:T(8,128)(2,1)} %cot_hbm.1, s32[1,3392]{1,0:T(1,128)S(1)} %reshape.7.degree_ref, s32[424,848]{1,0:T(8,128)} %bitcast.1, bf16[424,512]{1,0:T(8,128)(2,1)} %f_hbm.1, bf16[512,512]{1,0:T(8,128)(2,1)} %w_hbm.1), custom_call_target="tpu_custom_call" | custom-call | tf_op jit(solution)/shard_map/pallas_call | solution.py:228
  34.1 0.6 %copy.9 = bf16[424,128]{1,0:T(8,128)(2,1)} copy(bf16[424,128]{1,0:T(8,128)(2,1)S(1)} %get-tuple-element.4) | data formatting | bytes 217088
  34.7 0.6 %copy.10 = f32[64,128]{1,0:T(8,128)} copy(f32[64,128]{1,0:T(8,128)S(1)} %get-tuple-element.5) | data formatting | bytes 65536

commit v4 on v3

--- a/solution.py
+++ b/solution.py
@@ -38,7 +38,11 @@
     y, k = r // CORES, r % CORES
     o, i = c // I, c % I
     mate = y * CORES + (1 - k)
-    outer = [lax.rem(o + d, O) * I + i for d in range(1, O)]
+    if O == 4:
+        near = [1 + o % 2, (2 + 3 * o) % 5, 3 - 3 * (o // 2)]
+    else:
+        near = [(o + d) % O for d in range(1, O)]
+    outer = [p * I + i for p in near]
     inner = [o * I + lax.rem(i + d, I) for d in range(1, I)]
     others = [lax.rem(c + d, C) for d in range(1, C)]
     y_at = [lax.rem(y + 1 + s, Y) for s in range(Y)]
@@ -145,12 +149,13 @@
             def _(g):
                 mine[...] += term(0, g) + term(1, g)
 
-    for s in range(Y):
+    forward(0)
+    load_f.wait()
+    ft[...] = f_v[...].astype(F32).T.astype(BF16)
+    col_scale = scale_column(c * n, n)
+    for s in range(1, Y):
         forward(s)
-        if s == 0:
-            load_f.wait()
-            ft[...] = f_v[...].astype(F32).T.astype(BF16)
-            col_scale = scale_column(c * n, n)
+    for s in range(Y):
         gathered(s)
         if s == 0:
             swap.wait()

time: 35.9 us -> 33.7 us (0.939)
  Pallas kernels: 32.7 us -> 30.8 us
    pallas_call x1, Pallas kernels: 32.7 us -> 30.8 us  [per_device(): pl.pallas_call(functools.partial(kernel, R, C, block), out_shape=(jax.Sha...]
where the time goes in v4:
time: 33.7 us; the launch traced here: 33.5 us
  Pallas kernels  30.8 us (91%)
  local copies, waits for them, and re-layouts  1.99 us (6%)
  between operations  0.64 us (2%)
    pallas_call x1, Pallas kernels, per_device(): pl.pallas_call(functools.partial(kernel, R, C, block), out_shape=(jax.Sha...  30.8 us
    unnamed x2, local copies, waits for them, and re-layouts  1.26 us
    reshape x1, local copies, waits for them, and re-layouts, per_device(): degree.reshape(1, nodes)  0.73 us

profile of v4, /device:TPU:0, one launch (start us, length us, event | category | flops | bytes accessed | tf_op | source)
XLA Modules:
  0.0 33.5 jit_solution(17018897654015075527)
XLA Ops:
  0.6 0.7 %reshape.7.degree_ref = s32[1,3392]{1,0:T(1,128)S(1)} reshape(s32[3392]{0:T(1024)} %param.6) | data formatting | bytes 27136 | tf_op jit(solution)/shard_map/reshape | solution.py:274
  1.4 30.8 %shard_map.68 = (bf16[424,128]{1,0:T(8,128)(2,1)S(1)}, f32[64,128]{1,0:T(8,128)S(1)}) custom-call(bf16[106,512]{1,0:T(8,128)(2,1)} %cot_hbm.1, s32[1,3392]{1,0:T(1,128)S(1)} %reshape.7.degree_ref, s32[424,848]{1,0:T(8,128)} %bitcast.1, bf16[424,512]{1,0:T(8,128)(2,1)} %f_hbm.1, bf16[512,512]{1,0:T(8,128)(2,1)} %w_hbm.1), custom_call_target="tpu_custom_call" | custom-call | tf_op jit(solution)/shard_map/pallas_call | solution.py:233
  32.2 0.6 %copy.9 = bf16[424,128]{1,0:T(8,128)(2,1)} copy(bf16[424,128]{1,0:T(8,128)(2,1)S(1)} %get-tuple-element.4) | data formatting | bytes 217088
  32.9 0.6 %copy.10 = f32[64,128]{1,0:T(8,128)} copy(f32[64,128]{1,0:T(8,128)S(1)} %get-tuple-element.5) | data formatting | bytes 65536

commit v5 on v4

--- a/solution.py
+++ b/solution.py
@@ -161,7 +161,7 @@
             swap.wait()
         product(s)
         if s < Y - 1:
-            part[s] = mine[...]
+            part[s] = mine[...].astype(BF16)
             remote(
                 part.at[s], theirs.at[s], part_send.at[s], part_recv.at[s], y_at[s] * CORES + k, c
             ).start()
@@ -169,7 +169,7 @@
     total = mine[...]
     for s in range(Y - 1):
         await_bytes(theirs.at[s], part_recv.at[s])
-        total = total + theirs[s]
+        total = total + theirs[s].astype(F32)
     z_mine = (total * col_scale).astype(BF16)
     z_all[r] = z_mine
     z_here = z_all.at[r]
@@ -249,8 +249,8 @@
             pltpu.VMEM((width, n), BF16),
             pltpu.VMEM((Y, CORES, C, slot, share), BF16),
             pltpu.VMEM((n, share), F32),
-            pltpu.VMEM((max(Y - 1, 1), n, share), F32),
-            pltpu.VMEM((max(Y - 1, 1), n, share), F32),
+            pltpu.VMEM((max(Y - 1, 1), n, share), BF16),
+            pltpu.VMEM((max(Y - 1, 1), n, share), BF16),
             pltpu.VMEM((R, n, share), BF16),
             pltpu.VMEM((C, width // C, share), F32),
             pltpu.VMEM((C, width // C, share), F32),

time: 33.7 us -> 32.9 us (0.976)
  Pallas kernels: 30.8 us -> 30 us
    pallas_call x1, Pallas kernels: 30.8 us -> 30 us  [per_device(): pl.pallas_call(functools.partial(kernel, R, C, block), out_shape=(jax.Sha...]
where the time goes in v5:
time: 32.9 us; the launch traced here: 32.7 us
  Pallas kernels  30 us (91%)
  local copies, waits for them, and re-layouts  1.99 us (6%)
  between operations  0.64 us (2%)
    pallas_call x1, Pallas kernels, per_device(): pl.pallas_call(functools.partial(kernel, R, C, block), out_shape=(jax.Sha...  30 us
    unnamed x2, local copies, waits for them, and re-layouts  1.26 us
    reshape x1, local copies, waits for them, and re-layouts, per_device(): degree.reshape(1, nodes)  0.73 us

profile of v5, /device:TPU:0, one launch (start us, length us, event | category | flops | bytes accessed | tf_op | source)
XLA Modules:
  0.0 32.7 jit_solution(11296166608486624427)
XLA Ops:
  0.6 0.7 %reshape.7.degree_ref = s32[1,3392]{1,0:T(1,128)S(1)} reshape(s32[3392]{0:T(1024)} %param.6) | data formatting | bytes 27136 | tf_op jit(solution)/shard_map/reshape | solution.py:274
  1.4 30.0 %shard_map.68 = (bf16[424,128]{1,0:T(8,128)(2,1)S(1)}, f32[64,128]{1,0:T(8,128)S(1)}) custom-call(bf16[106,512]{1,0:T(8,128)(2,1)} %cot_hbm.1, s32[1,3392]{1,0:T(1,128)S(1)} %reshape.7.degree_ref, s32[424,848]{1,0:T(8,128)} %bitcast.1, bf16[424,512]{1,0:T(8,128)(2,1)} %f_hbm.1, bf16[512,512]{1,0:T(8,128)(2,1)} %w_hbm.1), custom_call_target="tpu_custom_call" | custom-call | tf_op jit(solution)/shard_map/pallas_call | solution.py:233
  31.4 0.6 %copy.9 = bf16[424,128]{1,0:T(8,128)(2,1)} copy(bf16[424,128]{1,0:T(8,128)(2,1)S(1)} %get-tuple-element.4) | data formatting | bytes 217088
  32.1 0.6 %copy.10 = f32[64,128]{1,0:T(8,128)} copy(f32[64,128]{1,0:T(8,128)S(1)} %get-tuple-element.5) | data formatting | bytes 65536
